TPU v7x, 32 devices: a whole 2x2x4 slice. The times are simulated.
32 devices in a mesh: dp: 2 (over x), expert: 8 (over z, core), tensor: 2 (over y).
Axes of the slice: x: 2, y: 2, z: 4, core: 2. Of those that a mesh axis runs over, the one named last changes fastest.
Arguments:
- tokens: bfloat16 [192, 256, 1280], P(('dp', 'expert', 'tensor')), may hold values from -16 to 16
- cotangent: bfloat16 [192, 256, 1280], P(('dp', 'expert', 'tensor')), may hold values from -6 to 6
- norm_gain: float32 [1280], replicated, may hold values from 0.5 to 1.5
- slot_keys: bfloat16 [1280, 16], replicated, may hold values from -2 to 2
- w_in: bfloat16 [8, 1280, 2560], P('expert', None, 'tensor'), may hold values from -0.15625 to 0.15625
- w_out: bfloat16 [8, 2560, 1280], P('expert', 'tensor'), may hold values from -0.125 to 0.125
Outputs:
- grad_tokens: bfloat16 [192, 256, 1280], P(('dp', 'expert', 'tensor'))
- grad_gain: float32 [1280], replicated
- grad_keys: float32 [1280, 16], replicated
- grad_in: bfloat16 [8, 1280, 2560], P('expert', 'dp', 'tensor')
- grad_out: bfloat16 [8, 2560, 1280], P('expert', 'tensor', 'dp')
All inputs are finite; a program needn't handle non-finite values.
Results may differ from a plain program's by a relative error of at most 0.014.
The roundings to bfloat16 on the way count: a program that leaves them out, or rounds other values in their place, can miss the bound.
Values may be sent and summed in bfloat16 or wider, within the bound.
A program may use at most 128 MiB of HBM per device.

v0:
```python
import jax
import jax.numpy as jnp
from jax import lax
from jax.sharding import PartitionSpec as P

SLOT_PER = 2
EPSILON = 1e-06


def mixing_forward(tokens, gain, slot_keys):
    average = jnp.mean(tokens, axis=-1, keepdims=True, dtype=jnp.float32)
    centred = tokens.astype(jnp.float32) - average
    spread = jnp.mean(centred * centred, axis=-1, keepdims=True)
    inverse = lax.rsqrt(spread + EPSILON)
    scaled = centred * inverse
    normed = (scaled * gain).astype(jnp.bfloat16)
    logits = jnp.einsum("bmd,dn->bmn", normed, slot_keys, preferred_element_type=jnp.float32)
    dispatch = jax.nn.softmax(logits, axis=1)
    combine = jax.nn.softmax(logits, axis=2)
    dispatch_low = dispatch.astype(jnp.bfloat16)
    slot_values = jnp.einsum(
        "bmn,bmd->bnd", dispatch_low, normed, preferred_element_type=jnp.float32
    )
    return (slot_values, combine, (scaled, inverse, normed, dispatch, combine, dispatch_low))


def mixing_backward(saved, gain, slot_keys, slot_grad, combine_grad):
    scaled, inverse, normed, dispatch, combine, dispatch_low = saved
    grad_dispatch = jnp.einsum(
        "bnd,bmd->bmn", slot_grad, normed, preferred_element_type=jnp.float32
    )
    grad_normed = jnp.einsum(
        "bmn,bnd->bmd", dispatch_low, slot_grad, preferred_element_type=jnp.float32
    )
    grad_logits = dispatch * (
        grad_dispatch - jnp.sum(dispatch * grad_dispatch, axis=1, keepdims=True)
    )
    grad_logits = grad_logits + combine * (
        combine_grad - jnp.sum(combine * combine_grad, axis=2, keepdims=True)
    )
    keys_wide = slot_keys.astype(jnp.float32)
    grad_normed = grad_normed + jnp.einsum(
        "bmn,dn->bmd", grad_logits, keys_wide, precision=lax.Precision.HIGHEST
    )
    keys_term = jnp.einsum(
        "bmd,bmn->dn", normed.astype(jnp.float32), grad_logits, precision=lax.Precision.HIGHEST
    )
    gain_term = jnp.sum(grad_normed * scaled, axis=(0, 1))
    grad_scaled = grad_normed * gain
    first_mean = jnp.mean(grad_scaled, axis=-1, keepdims=True)
    second_mean = jnp.mean(grad_scaled * scaled, axis=-1, keepdims=True)
    grad_tok = inverse * (grad_scaled - first_mean - scaled * second_mean)
    return (grad_tok, gain_term, keys_term)


def contract_rows(left, right):
    return lax.dot_general(
        left, right, (((0,), (0,)), ((), ())), preferred_element_type=jnp.float32
    )


def contract_cols(left, right):
    return lax.dot_general(
        left, right, (((1,), (1,)), ((), ())), preferred_element_type=jnp.float32
    )


def local(tokens, cotangent, norm_gain, slot_keys, w_in, w_out):
    local_imgs, token_count, features = tokens.shape
    slot_count = slot_keys.shape[1]
    experts = slot_count // SLOT_PER
    slot_values, combine, saved = mixing_forward(tokens, norm_gain, slot_keys)
    slot_inputs = slot_values.astype(jnp.bfloat16).reshape(local_imgs, experts, SLOT_PER, features)
    arrived = lax.all_to_all(slot_inputs, "expert", split_axis=1, concat_axis=0, tiled=True)
    slot_rows = lax.all_gather(arrived, "tensor", axis=0, tiled=True).reshape(-1, features)
    first_proj = w_in[0]
    second_proj = w_out[0]
    pre_act = jnp.dot(slot_rows, first_proj, preferred_element_type=jnp.float32)
    hidden = jax.nn.gelu(pre_act).astype(jnp.bfloat16)
    segment = hidden
    outputs = lax.psum_scatter(
        jnp.dot(segment, second_proj, preferred_element_type=jnp.float32),
        "tensor",
        scatter_dimension=0,
        tiled=True,
    )
    outputs = outputs.astype(jnp.bfloat16).reshape(arrived.shape)
    returned = lax.all_to_all(outputs, "expert", split_axis=0, concat_axis=1, tiled=True).reshape(
        local_imgs, slot_count, features
    )
    combine_low = combine.astype(jnp.bfloat16)
    grad_slots = jnp.einsum(
        "bmn,bmd->bnd", combine_low, cotangent, preferred_element_type=jnp.float32
    )
    grad_slots = grad_slots.astype(jnp.bfloat16).reshape(local_imgs, experts, SLOT_PER, features)
    grad_combine = jnp.einsum(
        "bmd,bnd->bmn", cotangent, returned, preferred_element_type=jnp.float32
    )
    grads_sent = lax.all_to_all(grad_slots, "expert", split_axis=1, concat_axis=0, tiled=True)
    grad_rows = lax.all_gather(grads_sent, "tensor", axis=0, tiled=True).reshape(-1, features)
    grad_hidden = contract_cols(grad_rows, second_proj)
    grad_pre = jax.vjp(jax.nn.gelu, pre_act)[1](grad_hidden)[0].astype(jnp.bfloat16)
    segment = grad_pre
    grad_in_rows = lax.psum_scatter(
        contract_cols(segment, first_proj), "tensor", scatter_dimension=0, tiled=True
    )
    grad_in_rows = grad_in_rows.astype(jnp.bfloat16).reshape(arrived.shape)
    grad_back = lax.all_to_all(
        grad_in_rows, "expert", split_axis=0, concat_axis=1, tiled=True
    ).reshape(local_imgs, slot_count, features)
    grad_tok, gain_term, keys_term = mixing_backward(
        saved, norm_gain, slot_keys, grad_back, grad_combine
    )
    grad_tokens = (cotangent.astype(jnp.float32) + grad_tok).astype(jnp.bfloat16)
    grad_gain, grad_keys = lax.psum((gain_term, keys_term), ("dp", "expert", "tensor"))
    split_rows, split_grads = (
        lax.all_to_all(slot_rows, "dp", split_axis=1, concat_axis=0, tiled=True),
        lax.all_to_all(grad_rows, "dp", split_axis=1, concat_axis=0, tiled=True),
    )
    first_total = contract_rows(split_rows, lax.all_gather(grad_pre, "dp", axis=0, tiled=True))
    second_total = contract_rows(lax.all_gather(hidden, "dp", axis=0, tiled=True), split_grads)
    return (
        grad_tokens,
        grad_gain,
        grad_keys,
        first_total.astype(jnp.bfloat16)[None],
        second_total.astype(jnp.bfloat16)[None],
    )


def solution(mesh):
    placed = (
        P(("dp", "expert", "tensor"), None, None),
        P(("dp", "expert", "tensor"), None, None),
        P(),
        P(),
        P("expert", None, "tensor"),
        P("expert", "tensor", None),
    )
    return jax.shard_map(
        local,
        mesh=mesh,
        in_specs=placed,
        out_specs=(
            P(("dp", "expert", "tensor"), None, None),
            P(),
            P(),
            P("expert", "dp", "tensor"),
            P("expert", "tensor", "dp"),
        ),
        check_vma=False,
    )
```

profile of v0, /device:TPU:8, one launch (start us, length us, event | category | flops | bytes accessed | tf_op | source)
XLA Modules:
  0.0 315.5 jit_solution(6597556359371723776)
XLA Ops:
  7.2 2.8 convert_reduce_fusion
  10.1 3.4 %fusion.15 = f32[6,256]{1,0:T(8,128)S(1)} fusion(bf16[6,256,1280]{2,1,0:T(8,128)(2,1)} %param.6, f32[6,256]{1,0:T(8,128)S(1)} %broadcast_multiply_fusion.2), kind=kLoop, calls=%fused_computation.17 | loop fusion | flops 7862784 | bytes 3944448 | tf_op jit(solution)/shard_map/reduce_sum | solution.py:13
  15.9 4.2 %convolution_convert_fusion.2 = bf16[6,16,1280]{2,1,0:T(8,128)(2,1)} fusion(f32[6,16]{1,0:T(8,128)S(1)} %get-tuple-element.8, f32[6,256,16]{1,2,0:T(8,128)S(1)} %fusion.41, bf16[6,256,1280]{2,1,0:T(8,128)(2,1)} %param.6, f32[1280]{0:T(1024)S(1)} %copy-done.6, f32[6,256]{1,0:T(8,128)S(1)} %add_rsqrt_fusion, f32[6,256]{1,0:T(8,128)S(1)} %broadcast_multiply_fusion.2), kind=kOutput, calls=%fused_computation.32 | convolution fusion | flops 72941920 | bytes 4294016 | tf_op jit(solution)/shard_map/bmn,bmd->bnd/dot_general | solution.py:21
  22.0 5.3 %all-to-all-start.1 = ((bf16[6,8,2,1280]{3,2,0,1:T(2,128)(2,1)}), bf16[6,8,2,1280]{3,2,0,1:T(2,128)(2,1)S(1)}, u32[]{:S(2)}, u32[]{:S(2)}) async-start(bf16[6,8,2,1280]{3,2,0,1:T(2,128)(2,1)} %copy.39), calls=%async_computation.1 | async-start | bytes 491520 | tf_op jit(solution)/shard_map/all_to_all | solution.py:74
  28.9 3.5 %convolution_convert_fusion.3 = bf16[6,16,1280]{2,1,0:T(8,128)(2,1)} fusion(bf16[6,256,1280]{2,1,0:T(8,128)(2,1)} %param.7, f32[6,256]{1,0:T(8,128)S(1)} %get-tuple-element.10, f32[6,256,16]{1,2,0:T(8,128)} %copy-done.3), kind=kOutput, calls=%fused_computation.33 | convolution fusion | flops 63112720 | bytes 4282368 | tf_op jit(solution)/shard_map/bmn,bmd->bnd/dot_general | solution.py:92
  36.0 5.1 %all-to-all-start = ((bf16[6,8,2,1280]{3,2,0,1:T(2,128)(2,1)}), bf16[6,8,2,1280]{3,2,0,1:T(2,128)(2,1)}, u32[]{:S(2)}, u32[]{:S(2)}) async-start(bf16[6,8,2,1280]{3,2,0,1:T(2,128)(2,1)} %copy.37), calls=%async_computation | async-start | bytes 491520 | tf_op jit(solution)/shard_map/all_to_all | solution.py:99
  41.1 8.7 %all_gather.13 = bf16[96,1,2,1280]{3,2,1,0:T(2,128)(2,1)} all-gather(bf16[48,1,2,1280]{3,2,1,0:T(2,128)(2,1)S(1)} %bitcast.84), channel_id=1, replica_groups=mesh['dp'=2,'expert'=8,'tensor'=2] {'tensor'}, dimensions={0}, use_global_device_ids=true | all-gather | bytes 737280 | tf_op jit(solution)/shard_map/all_gather | solution.py:75
  49.9 2.0 reshape.74
  51.9 10.7 %all_gather.12 = bf16[96,1,2,1280]{3,2,1,0:T(2,128)(2,1)} all-gather(bf16[48,1,2,1280]{3,2,1,0:T(2,128)(2,1)} %bitcast.4), channel_id=1, replica_groups=mesh['dp'=2,'expert'=8,'tensor'=2] {'tensor'}, dimensions={0}, use_global_device_ids=true | all-gather | bytes 737280 | tf_op jit(solution)/shard_map/all_gather | solution.py:100
  62.6 2.0 reshape.72
  64.6 2.7 multiply_convert_fusion
  67.3 3.5 %fusion.36 = bf16[192,1280]{1,0:T(8,128)(2,1)S(1)} fusion(f32[192,1280]{1,0:T(8,128)S(1)} %get-tuple-element.13, bf16[192,1280]{1,0:T(8,128)(2,1)} %reshape.72, bf16[1,1280,1280]{2,1,0:T(8,128)(2,1)} %param.11), kind=kOutput, calls=%fused_computation.48 | convolution fusion | flops 634060800 | bytes 5242880 | tf_op jit(solution)/shard_map/dot_general | solution.py:63
  71.6 2.2 fusion.16
  73.8 3.8 %fusion.20 = f32[192,1280]{1,0:T(8,128)} fusion(bf16[192,1280]{1,0:T(8,128)(2,1)} %get-tuple-element.12, bf16[1,1280,1280]{2,1,0:T(8,128)(2,1)} %param.11), kind=kOutput, calls=%fused_computation.24 | convolution fusion | flops 629145600 | bytes 4751360 | tf_op jit(solution)/shard_map/dot_general | solution.py:82
  77.7 2.1 all_to_all.90
  79.8 2.2 all_to_all.94
  83.9 4.2 %all-to-all-start.4 = ((bf16[192,2,640]{2,0,1:T(8,128)(2,1)}), bf16[192,2,640]{2,0,1:T(8,128)(2,1)}, u32[]{:S(2)}, u32[]{:S(2)}) async-start(bf16[192,2,640]{2,0,1:T(8,128)(2,1)} %copy.45), calls=%async_computation.6 | async-start | bytes 983040 | tf_op jit(solution)/shard_map/all_to_all | solution.py:117
  90.0 15.4 %all_gather.14 = bf16[384,1280]{1,0:T(8,128)(2,1)} all-gather(bf16[192,1280]{1,0:T(8,128)(2,1)} %copy-done.2), channel_id=1, replica_groups=mesh['dp'=2,'expert'=8,'tensor'=2] {'dp'}, dimensions={0}, use_global_device_ids=true | all-gather | bytes 1474560 | tf_op jit(solution)/shard_map/all_gather | solution.py:120
  105.4 4.2 %all-to-all-start.5 = ((bf16[192,2,640]{2,0,1:T(8,128)(2,1)}), bf16[192,2,640]{2,0,1:T(8,128)(2,1)}, u32[]{:S(2)}, u32[]{:S(2)}) async-start(bf16[192,2,640]{2,0,1:T(8,128)(2,1)} %copy.46), calls=%async_computation.7 | async-start | bytes 983040 | tf_op jit(solution)/shard_map/all_to_all | solution.py:118
  109.6 17.4 %all_gather.15 = bf16[384,1280]{1,0:T(8,128)(2,1)} all-gather(bf16[192,1280]{1,0:T(8,128)(2,1)} %get-tuple-element.12), channel_id=1, replica_groups=mesh['dp'=2,'expert'=8,'tensor'=2] {'dp'}, dimensions={0}, use_global_device_ids=true | all-gather | bytes 1474560 | tf_op jit(solution)/shard_map/all_gather | solution.py:121
  128.9 5.1 %all-to-all-start.2 = ((bf16[48,1,2,1280]{3,2,1,0:T(2,128)(2,1)}), bf16[48,1,2,1280]{3,2,1,0:T(2,128)(2,1)S(1)}, u32[]{:S(2)}, u32[]{:S(2)}) async-start(bf16[48,1,2,1280]{3,2,1,0:T(2,128)(2,1)} %bitcast.85), calls=%async_computation.3 | async-start | bytes 491520 | tf_op jit(solution)/shard_map/all_to_all | solution.py:108
  133.9 3.6 %fusion.24 = bf16[1,640,1280]{2,1,0:T(8,128)(2,1)} fusion(bf16[384,640]{1,0:T(8,128)(2,1)} %bitcast.20, bf16[384,1280]{1,0:T(8,128)(2,1)} %all_gather.14), kind=kOutput, calls=%fused_computation.30 | convolution fusion | flops 629964800 | bytes 3112960 | tf_op jit(solution)/shard_map/dot_general | solution.py:57
  137.5 3.6 %fusion.25 = bf16[1,1280,640]{2,1,0:T(8,128)(2,1)} fusion(bf16[384,1280]{1,0:T(8,128)(2,1)} %all_gather.15, bf16[384,640]{1,0:T(8,128)(2,1)} %bitcast.23), kind=kOutput, calls=%fused_computation.31 | convolution fusion | flops 629964800 | bytes 3112960 | tf_op jit(solution)/shard_map/dot_general | solution.py:57
  144.6 5.1 %all-to-all-start.3 = ((bf16[48,1,2,1280]{3,2,1,0:T(2,128)(2,1)}), bf16[48,1,2,1280]{3,2,1,0:T(2,128)(2,1)}, u32[]{:S(2)}, u32[]{:S(2)}) async-start(bf16[48,1,2,1280]{3,2,1,0:T(2,128)(2,1)} %bitcast.86), calls=%async_computation.5 | async-start | bytes 491520 | tf_op jit(solution)/shard_map/all_to_all | solution.py:88
  151.7 4.1 %multiply_reduce_fusion.2 = (f32[6,16]{1,0:T(8,128)S(1)}, f32[6,256,16]{1,2,0:T(8,128)}) fusion(f32[6,256,16]{1,2,0:T(8,128)} %get-tuple-element.9, f32[6,16]{1,0:T(8,128)S(1)} %get-tuple-element.8, bf16[6,16,1280]{2,1,0:T(8,128)(2,1)S(1)} %reshape.76, bf16[6,256,1280]{2,1,0:T(8,128)(2,1)} %param.6, f32[1280]{0:T(1024)} %param.8, ...), kind=kOutput, calls=%fused_computation.54 | convolution fusion | flops 72818592 | bytes 4392704 | tf_op jit(solution)/shard_map/bnd,bmd->bmn/dot_general | solution.py:29
  155.8 5.4 %fusion.43 = f32[6,256,1280]{2,1,0:T(8,128)} fusion(bf16[6,16,1280]{2,1,0:T(8,128)(2,1)S(1)} %reshape.76, f32[6,16]{1,0:T(8,128)S(1)} %get-tuple-element.8, f32[6,256,16]{1,2,0:T(8,128)} %copy-done.3), kind=kOutput, calls=%fused_computation.61 | convolution fusion | flops 62988640 | bytes 8208768 | tf_op jit(solution)/shard_map/bmn,bnd->bmd/dot_general | solution.py:32
  164.0 3.3 %multiply_reduce_fusion.1 = (f32[6,256]{1,0:T(8,128)S(1)}, f32[6,256,16]{1,2,0:T(8,128)S(1)}) fusion(f32[6,256,16]{1,2,0:T(8,128)} %get-tuple-element.11, f32[6,256]{1,0:T(8,128)S(1)} %get-tuple-element.10, bf16[6,16,1280]{2,1,0:T(8,128)(2,1)S(1)} %reshape.78, bf16[6,256,1280]{2,1,0:T(8,128)(2,1)} %param.7), kind=kOutput, calls=%fused_computation.53 | convolution fusion | flops 62986752 | bytes 4386816 | tf_op jit(solution)/shard_map/bmd,bnd->bmn/dot_general | solution.py:96
  168.4 4.5 %convolution_bitcast_fusion = f32[1280,16]{0,1:T(8,128)} fusion(f32[6,256,16]{1,2,0:T(8,128)S(1)} %multiply_add_fusion, bf16[6,256,1280]{2,1,0:T(8,128)(2,1)} %param.6, f32[1280]{0:T(1024)} %param.8, f32[6,256]{1,0:T(8,128)S(1)} %add_rsqrt_fusion, f32[6,256]{1,0:T(8,128)S(1)} %broadcast_multiply_fusion.2), kind=kOutput, calls=%fused_computation.34 | convolution fusion | flops 387317760 | bytes 4129792 | tf_op jit(solution)/shard_map/bmd,bmn->dn/dot_general | solution.py:45
  172.9 10.6 %fusion.14 = (f32[1280]{0:T(1024)S(1)}, f32[6,256]{1,0:T(8,128)S(1)}, f32[6,256]{1,0:T(8,128)S(1)}, f32[6,256,1280]{2,1,0:T(8,128)}) fusion(bf16[6,256,1280]{2,1,0:T(8,128)(2,1)} %param.6, f32[6,256]{1,0:T(8,128)S(1)} %add_rsqrt_fusion, f32[6,256]{1,0:T(8,128)S(1)} %broadcast_multiply_fusion.2, f32[1280]{0:T(1024)S(1)} %copy-done.7, ...), kind=kOutput, calls=%fused_computation.16 | convolution fusion | flops 397143808 | bytes 19834880 | tf_op jit(solution)/shard_map/bmn,dn->bmd/dot_general | solution.py:42
  183.5 8.4 %fusion.13 = bf16[6,256,1280]{2,1,0:T(8,128)(2,1)} fusion(bf16[6,256,1280]{2,1,0:T(8,128)(2,1)} %param.6, bf16[6,256,1280]{2,1,0:T(8,128)(2,1)} %param.7, f32[6,256,1280]{2,1,0:T(8,128)} %get-tuple-element.18, f32[6,256]{1,0:T(8,128)S(1)} %get-tuple-element.19, f32[6,256]{1,0:T(8,128)S(1)} %get-tuple-element.20, f32[1280]{0:T(1024)S(1)} %copy-done.7, ...), kind=kLoop, calls=%fused_computation.15 | loop fusion | flops 21626880 | bytes 19690496 | tf_op jit(solution)/shard_map/convert_element_type | solution.py:114
  191.9 39.3 %psum.14 = f32[1280]{0:T(1024)} all-reduce(f32[1280]{0:T(1024)S(1)} %get-tuple-element.5), channel_id=1, replica_groups=mesh['dp'=2,'expert'=8,'tensor'=2] {'dp','expert','tensor'}, use_global_device_ids=true, to_apply=%region_13.0 | all-reduce | flops 1280 | bytes 10240 | tf_op jit(solution)/shard_map/psum | solution.py:115
  231.2 76.2 %all-reduce.2.cloned.1.call-done = f32[1280,16]{0,1:T(8,128)} async-done(((f32[1280,16]{0,1:T(8,128)}), f32[1280,16]{0,1:T(8,128)}) %all-reduce.2.cloned.1.call-update) | async-done | bytes 81936 | tf_op jit(solution)/shard_map/psum | solution.py:115
  (52 shorter events, 26.8 us)
Async XLA Ops:
  7.2 57.4 %copy-start = (bf16[1,1280,1280]{2,1,0:T(8,128)(2,1)S(1)}, bf16[1,1280,1280]{2,1,0:T(8,128)(2,1)}, u32[]{:S(2)}) copy-start(bf16[1,1280,1280]{2,1,0:T(8,128)(2,1)} %param.10) | copy-start | bytes 9830404
  7.2 6.3 %copy-start.1 = (bf16[6,256,1280]{2,1,0:T(8,128)(2,1)S(1)}, bf16[6,256,1280]{2,1,0:T(8,128)(2,1)}, u32[]{:S(2)}) copy-start(bf16[6,256,1280]{2,1,0:T(8,128)(2,1)} %param.6) | copy-start | bytes 11796484
  7.2 6.3 %copy-start.6 = (f32[1280]{0:T(1024)S(1)}, f32[1280]{0:T(1024)}, u32[]{:S(2)}) copy-start(f32[1280]{0:T(1024)} %param.8) | copy-start | bytes 15364
  7.2 6.3 %copy-start.4 = (bf16[1280,16]{0,1:T(8,128)(2,1)S(1)}, bf16[1280,16]{0,1:T(8,128)(2,1)}, u32[]{:S(2)}) copy-start(bf16[1280,16]{0,1:T(8,128)(2,1)} %param.9) | copy-start | bytes 122884
  15.1 0.8 copy-start.3
  22.0 14.0 %all-to-all-start.1 = ((bf16[6,8,2,1280]{3,2,0,1:T(2,128)(2,1)}), bf16[6,8,2,1280]{3,2,0,1:T(2,128)(2,1)S(1)}, u32[]{:S(2)}, u32[]{:S(2)}) async-start(bf16[6,8,2,1280]{3,2,0,1:T(2,128)(2,1)} %copy.39), calls=%async_computation.1 | async-start | bytes 491520 | tf_op jit(solution)/shard_map/all_to_all | solution.py:74
  36.0 15.8 %all-to-all-start = ((bf16[6,8,2,1280]{3,2,0,1:T(2,128)(2,1)}), bf16[6,8,2,1280]{3,2,0,1:T(2,128)(2,1)}, u32[]{:S(2)}, u32[]{:S(2)}) async-start(bf16[6,8,2,1280]{3,2,0,1:T(2,128)(2,1)} %copy.37), calls=%async_computation | async-start | bytes 491520 | tf_op jit(solution)/shard_map/all_to_all | solution.py:99
  41.1 85.9 %reduce-scatter.3.cloned.1.call-start = ((), (), s32[]{:S(2)}) async-start(), calls=%async_computation.8 | async-start | bytes 1474560 | tf_op jit(solution)/shard_map/reduce_scatter | solution.py:104
  70.8 0.8 copy-start.2
  73.8 67.4 %reduce-scatter.5.cloned.1.call-start = ((), (), s32[]{:S(2)}) async-start(), calls=%async_computation.9 | async-start | bytes 1474560 | tf_op jit(solution)/shard_map/reduce_scatter | solution.py:81
  83.9 21.5 %all-to-all-start.4 = ((bf16[192,2,640]{2,0,1:T(8,128)(2,1)}), bf16[192,2,640]{2,0,1:T(8,128)(2,1)}, u32[]{:S(2)}, u32[]{:S(2)}) async-start(bf16[192,2,640]{2,0,1:T(8,128)(2,1)} %copy.45), calls=%async_computation.6 | async-start | bytes 983040 | tf_op jit(solution)/shard_map/all_to_all | solution.py:117
  105.4 23.5 %all-to-all-start.5 = ((bf16[192,2,640]{2,0,1:T(8,128)(2,1)}), bf16[192,2,640]{2,0,1:T(8,128)(2,1)}, u32[]{:S(2)}, u32[]{:S(2)}) async-start(bf16[192,2,640]{2,0,1:T(8,128)(2,1)} %copy.46), calls=%async_computation.7 | async-start | bytes 983040 | tf_op jit(solution)/shard_map/all_to_all | solution.py:118
  128.9 15.8 %all-to-all-start.2 = ((bf16[48,1,2,1280]{3,2,1,0:T(2,128)(2,1)}), bf16[48,1,2,1280]{3,2,1,0:T(2,128)(2,1)S(1)}, u32[]{:S(2)}, u32[]{:S(2)}) async-start(bf16[48,1,2,1280]{3,2,1,0:T(2,128)(2,1)} %bitcast.85), calls=%async_computation.3 | async-start | bytes 491520 | tf_op jit(solution)/shard_map/all_to_all | solution.py:108
  144.6 16.5 %all-to-all-start.3 = ((bf16[48,1,2,1280]{3,2,1,0:T(2,128)(2,1)}), bf16[48,1,2,1280]{3,2,1,0:T(2,128)(2,1)}, u32[]{:S(2)}, u32[]{:S(2)}) async-start(bf16[48,1,2,1280]{3,2,1,0:T(2,128)(2,1)} %bitcast.86), calls=%async_computation.5 | async-start | bytes 491520 | tf_op jit(solution)/shard_map/all_to_all | solution.py:88
  149.7 157.7 %all-reduce.2.cloned.1.call-start = ((), (), s32[]{:S(2)}) async-start(), calls=%async_computation.10 | async-start | bytes 163840 | tf_op jit(solution)/shard_map/psum | solution.py:115
  167.3 5.6 %copy-start.5 = (bf16[1280,16]{0,1:T(8,128)(2,1)S(1)}, bf16[1280,16]{0,1:T(8,128)(2,1)}, u32[]{:S(2)}) copy-start(bf16[1280,16]{0,1:T(8,128)(2,1)} %param.9) | copy-start | bytes 122884
  167.3 5.6 %copy-start.7 = (f32[1280]{0:T(1024)S(1)}, f32[1280]{0:T(1024)}, u32[]{:S(2)}) copy-start(f32[1280]{0:T(1024)} %param.8) | copy-start | bytes 15364
Sparse Core Ops, SparseCore 0:
  73.9 19.6 reduce-scatter.2
  96.4 19.6 reduce-scatter.4
  183.6 123.7 all-reduce.1
where the time goes:
time: 317 us; the launch traced here: 316 us
  blocking collectives  91.5 us (29%)
  waiting for transfers between devices  76.3 us (24%)
  matrix products  56.6 us (18%)
  starting transfers between devices  29.1 us (9%)
  local copies, waits for them, and re-layouts  27.1 us (9%)
  other arithmetic  21 us (7%)
  between operations  13.9 us (4%)
    psum x1, waiting for transfers between devices, local(): lax.psum((gain_term, keys_term), ('dp', 'expert', 'tensor'))  76.2 us
    psum x1, blocking collectives, local(): lax.psum((gain_term, keys_term), ('dp', 'expert', 'tensor'))  39.3 us
    all_gather x1, blocking collectives, local(): lax.all_gather(hidden, 'dp', axis=0, tiled=True)  17.4 us
    all_gather x1, blocking collectives, local(): lax.all_gather(grad_pre, 'dp', axis=0, tiled=True)  15.4 us
    all_gather x1, blocking collectives, local(): lax.all_gather(grads_sent, 'tensor', axis=0, tiled=True)  10.7 us
    dot_general x1, matrix products, mixing_backward(): jnp.einsum('bmn,dn->bmd', grad_logits, keys_wide, precision=lax.Precision...  10.6 us
    all_gather x1, blocking collectives, local(): lax.all_gather(arrived, 'tensor', axis=0, tiled=True).reshape(-1, features)  8.73 us
    convert_element_type x1, other arithmetic, local(): (cotangent.astype(jnp.float32) + grad_tok).astype(jnp.bfloat16)  8.39 us
  transfers between devices with their start and end apart: 9, of which 1 were waited for; matrix products, arithmetic and copies ran while one was open for 16% of the time, Pallas kernels for 0%

commit v1 on v0

--- a/solution.py
+++ b/solution.py
@@ -112,7 +112,7 @@
         saved, norm_gain, slot_keys, grad_back, grad_combine
     )
     grad_tokens = (cotangent.astype(jnp.float32) + grad_tok).astype(jnp.bfloat16)
-    grad_gain, grad_keys = lax.psum((gain_term, keys_term), ("dp", "expert", "tensor"))
+    grad_gain, grad_keys = lax.psum(lax.psum((gain_term, keys_term), ("expert", "tensor")), "dp")
     split_rows, split_grads = (
         lax.all_to_all(slot_rows, "dp", split_axis=1, concat_axis=0, tiled=True),
         lax.all_to_all(grad_rows, "dp", split_axis=1, concat_axis=0, tiled=True),

time: 317 us -> 328 us (1.035)
  the two profiles are of different devices: /device:TPU:8 before, /device:TPU:0 now
where the time goes in v1:
time: 328 us; the launch traced here: 326 us
  blocking collectives  92.3 us (28%)
  waiting for transfers between devices  87.4 us (27%)
  matrix products  56.6 us (17%)
  starting transfers between devices  28 us (9%)
  local copies, waits for them, and re-layouts  27 us (8%)
  other arithmetic  21 us (6%)
  between operations  14 us (4%)
    psum x1, waiting for transfers between devices, local(): lax.psum((gain_term, keys_term), ('expert', 'tensor'))  86.7 us
    psum x1, blocking collectives, local(): lax.psum((gain_term, keys_term), ('expert', 'tensor'))  32.9 us
    all_gather x1, blocking collectives, local(): lax.all_gather(hidden, 'dp', axis=0, tiled=True)  17.8 us
    all_gather x1, blocking collectives, local(): lax.all_gather(grad_pre, 'dp', axis=0, tiled=True)  15.8 us
    all_gather x1, blocking collectives, local(): lax.all_gather(grads_sent, 'tensor', axis=0, tiled=True)  11.1 us
    dot_general x1, matrix products, mixing_backward(): jnp.einsum('bmn,dn->bmd', grad_logits, keys_wide, precision=lax.Precision...  10.6 us
    all_gather x1, blocking collectives, local(): lax.all_gather(arrived, 'tensor', axis=0, tiled=True).reshape(-1, features)  9.08 us
    convert_element_type x1, other arithmetic, local(): (cotangent.astype(jnp.float32) + grad_tok).astype(jnp.bfloat16)  8.38 us
  transfers between devices with their start and end apart: 10, of which 2 were waited for; matrix products, arithmetic and copies ran while one was open for 16% of the time, Pallas kernels for 0%

profile of v1, /device:TPU:0, one launch (start us, length us, event | category | flops | bytes accessed | tf_op | source)
XLA Modules:
  0.0 326.3 jit_solution(10600549730287297328)
XLA Ops:
  7.2 2.8 convert_reduce_fusion
  10.1 3.4 %fusion.15 = f32[6,256]{1,0:T(8,128)S(1)} fusion(bf16[6,256,1280]{2,1,0:T(8,128)(2,1)} %param.6, f32[6,256]{1,0:T(8,128)S(1)} %broadcast_multiply_fusion.2), kind=kLoop, calls=%fused_computation.17 | loop fusion | flops 7862784 | bytes 3944448 | tf_op jit(solution)/shard_map/reduce_sum | solution.py:13
  15.9 4.2 %convolution_convert_fusion.2 = bf16[6,16,1280]{2,1,0:T(8,128)(2,1)} fusion(f32[6,16]{1,0:T(8,128)S(1)} %get-tuple-element.8, f32[6,256,16]{1,2,0:T(8,128)S(1)} %fusion.41, bf16[6,256,1280]{2,1,0:T(8,128)(2,1)} %param.6, f32[1280]{0:T(1024)S(1)} %copy-done.6, f32[6,256]{1,0:T(8,128)S(1)} %add_rsqrt_fusion, f32[6,256]{1,0:T(8,128)S(1)} %broadcast_multiply_fusion.2), kind=kOutput, calls=%fused_computation.32 | convolution fusion | flops 72941920 | bytes 4294016 | tf_op jit(solution)/shard_map/bmn,bmd->bnd/dot_general | solution.py:21
  22.0 6.4 %all-to-all-start.1 = ((bf16[6,8,2,1280]{3,2,0,1:T(2,128)(2,1)}), bf16[6,8,2,1280]{3,2,0,1:T(2,128)(2,1)S(1)}, u32[]{:S(2)}, u32[]{:S(2)}) async-start(bf16[6,8,2,1280]{3,2,0,1:T(2,128)(2,1)} %copy.39), calls=%async_computation.1 | async-start | bytes 491520 | tf_op jit(solution)/shard_map/all_to_all | solution.py:74
  30.0 3.5 %convolution_convert_fusion.3 = bf16[6,16,1280]{2,1,0:T(8,128)(2,1)} fusion(bf16[6,256,1280]{2,1,0:T(8,128)(2,1)} %param.7, f32[6,256]{1,0:T(8,128)S(1)} %get-tuple-element.10, f32[6,256,16]{1,2,0:T(8,128)} %copy-done.3), kind=kOutput, calls=%fused_computation.33 | convolution fusion | flops 63112720 | bytes 4282368 | tf_op jit(solution)/shard_map/bmn,bmd->bnd/dot_general | solution.py:92
  37.7 4.5 %all-to-all-start = ((bf16[6,8,2,1280]{3,2,0,1:T(2,128)(2,1)}), bf16[6,8,2,1280]{3,2,0,1:T(2,128)(2,1)}, u32[]{:S(2)}, u32[]{:S(2)}) async-start(bf16[6,8,2,1280]{3,2,0,1:T(2,128)(2,1)} %copy.37), calls=%async_computation | async-start | bytes 491520 | tf_op jit(solution)/shard_map/all_to_all | solution.py:99
  42.2 9.1 %all_gather.13 = bf16[96,1,2,1280]{3,2,1,0:T(2,128)(2,1)} all-gather(bf16[48,1,2,1280]{3,2,1,0:T(2,128)(2,1)S(1)} %bitcast.84), channel_id=1, replica_groups=mesh['dp'=2,'expert'=8,'tensor'=2] {'tensor'}, dimensions={0}, use_global_device_ids=true | all-gather | bytes 737280 | tf_op jit(solution)/shard_map/all_gather | solution.py:75
  51.3 2.0 reshape.74
  53.3 11.1 %all_gather.12 = bf16[96,1,2,1280]{3,2,1,0:T(2,128)(2,1)} all-gather(bf16[48,1,2,1280]{3,2,1,0:T(2,128)(2,1)} %bitcast.4), channel_id=1, replica_groups=mesh['dp'=2,'expert'=8,'tensor'=2] {'tensor'}, dimensions={0}, use_global_device_ids=true | all-gather | bytes 737280 | tf_op jit(solution)/shard_map/all_gather | solution.py:100
  66.3 2.7 multiply_convert_fusion
  69.0 3.5 %fusion.36 = bf16[192,1280]{1,0:T(8,128)(2,1)S(1)} fusion(f32[192,1280]{1,0:T(8,128)S(1)} %get-tuple-element.13, bf16[192,1280]{1,0:T(8,128)(2,1)} %reshape.72, bf16[1,1280,1280]{2,1,0:T(8,128)(2,1)} %param.11), kind=kOutput, calls=%fused_computation.48 | convolution fusion | flops 634060800 | bytes 5242880 | tf_op jit(solution)/shard_map/dot_general | solution.py:63
  73.3 2.2 fusion.16
  75.6 3.8 %fusion.20 = f32[192,1280]{1,0:T(8,128)} fusion(bf16[192,1280]{1,0:T(8,128)(2,1)} %get-tuple-element.12, bf16[1,1280,1280]{2,1,0:T(8,128)(2,1)} %param.11), kind=kOutput, calls=%fused_computation.24 | convolution fusion | flops 629145600 | bytes 4751360 | tf_op jit(solution)/shard_map/dot_general | solution.py:82
  79.4 2.1 all_to_all.90
  81.6 2.1 all_to_all.94
  85.6 4.2 %all-to-all-start.4 = ((bf16[192,2,640]{2,0,1:T(8,128)(2,1)}), bf16[192,2,640]{2,0,1:T(8,128)(2,1)}, u32[]{:S(2)}, u32[]{:S(2)}) async-start(bf16[192,2,640]{2,0,1:T(8,128)(2,1)} %copy.45), calls=%async_computation.6 | async-start | bytes 983040 | tf_op jit(solution)/shard_map/all_to_all | solution.py:117
  91.7 15.8 %all_gather.14 = bf16[384,1280]{1,0:T(8,128)(2,1)} all-gather(bf16[192,1280]{1,0:T(8,128)(2,1)} %copy-done.2), channel_id=1, replica_groups=mesh['dp'=2,'expert'=8,'tensor'=2] {'dp'}, dimensions={0}, use_global_device_ids=true | all-gather | bytes 1474560 | tf_op jit(solution)/shard_map/all_gather | solution.py:120
  107.5 4.2 %all-to-all-start.5 = ((bf16[192,2,640]{2,0,1:T(8,128)(2,1)}), bf16[192,2,640]{2,0,1:T(8,128)(2,1)}, u32[]{:S(2)}, u32[]{:S(2)}) async-start(bf16[192,2,640]{2,0,1:T(8,128)(2,1)} %copy.46), calls=%async_computation.7 | async-start | bytes 983040 | tf_op jit(solution)/shard_map/all_to_all | solution.py:118
  111.7 17.8 %all_gather.15 = bf16[384,1280]{1,0:T(8,128)(2,1)} all-gather(bf16[192,1280]{1,0:T(8,128)(2,1)} %get-tuple-element.12), channel_id=1, replica_groups=mesh['dp'=2,'expert'=8,'tensor'=2] {'dp'}, dimensions={0}, use_global_device_ids=true | all-gather | bytes 1474560 | tf_op jit(solution)/shard_map/all_gather | solution.py:121
  131.4 3.6 %all-to-all-start.2 = ((bf16[48,1,2,1280]{3,2,1,0:T(2,128)(2,1)}), bf16[48,1,2,1280]{3,2,1,0:T(2,128)(2,1)S(1)}, u32[]{:S(2)}, u32[]{:S(2)}) async-start(bf16[48,1,2,1280]{3,2,1,0:T(2,128)(2,1)} %bitcast.85), calls=%async_computation.3 | async-start | bytes 491520 | tf_op jit(solution)/shard_map/all_to_all | solution.py:108
  135.0 3.6 %fusion.24 = bf16[1,640,1280]{2,1,0:T(8,128)(2,1)} fusion(bf16[384,640]{1,0:T(8,128)(2,1)} %bitcast.20, bf16[384,1280]{1,0:T(8,128)(2,1)} %all_gather.14), kind=kOutput, calls=%fused_computation.30 | convolution fusion | flops 629964800 | bytes 3112960 | tf_op jit(solution)/shard_map/dot_general | solution.py:57
  138.6 3.6 %fusion.25 = bf16[1,1280,640]{2,1,0:T(8,128)(2,1)} fusion(bf16[384,1280]{1,0:T(8,128)(2,1)} %all_gather.15, bf16[384,640]{1,0:T(8,128)(2,1)} %bitcast.23), kind=kOutput, calls=%fused_computation.31 | convolution fusion | flops 629964800 | bytes 3112960 | tf_op jit(solution)/shard_map/dot_general | solution.py:57
  145.7 5.1 %all-to-all-start.3 = ((bf16[48,1,2,1280]{3,2,1,0:T(2,128)(2,1)}), bf16[48,1,2,1280]{3,2,1,0:T(2,128)(2,1)}, u32[]{:S(2)}, u32[]{:S(2)}) async-start(bf16[48,1,2,1280]{3,2,1,0:T(2,128)(2,1)} %bitcast.86), calls=%async_computation.5 | async-start | bytes 491520 | tf_op jit(solution)/shard_map/all_to_all | solution.py:88
  152.7 4.1 %multiply_reduce_fusion.2 = (f32[6,16]{1,0:T(8,128)S(1)}, f32[6,256,16]{1,2,0:T(8,128)}) fusion(f32[6,256,16]{1,2,0:T(8,128)} %get-tuple-element.9, f32[6,16]{1,0:T(8,128)S(1)} %get-tuple-element.8, bf16[6,16,1280]{2,1,0:T(8,128)(2,1)S(1)} %reshape.76, bf16[6,256,1280]{2,1,0:T(8,128)(2,1)} %param.6, f32[1280]{0:T(1024)} %param.8, ...), kind=kOutput, calls=%fused_computation.54 | convolution fusion | flops 72818592 | bytes 4392704 | tf_op jit(solution)/shard_map/bnd,bmd->bmn/dot_general | solution.py:29
  156.9 5.4 %fusion.43 = f32[6,256,1280]{2,1,0:T(8,128)} fusion(bf16[6,16,1280]{2,1,0:T(8,128)(2,1)S(1)} %reshape.76, f32[6,16]{1,0:T(8,128)S(1)} %get-tuple-element.8, f32[6,256,16]{1,2,0:T(8,128)} %copy-done.3), kind=kOutput, calls=%fused_computation.61 | convolution fusion | flops 62988640 | bytes 8208768 | tf_op jit(solution)/shard_map/bmn,bnd->bmd/dot_general | solution.py:32
  165.1 3.3 multiply_reduce_fusion.1
  169.5 4.5 %convolution_bitcast_fusion = f32[1280,16]{0,1:T(8,128)} fusion(f32[6,256,16]{1,2,0:T(8,128)S(1)} %multiply_add_fusion, bf16[6,256,1280]{2,1,0:T(8,128)(2,1)} %param.6, f32[1280]{0:T(1024)} %param.8, f32[6,256]{1,0:T(8,128)S(1)} %add_rsqrt_fusion, f32[6,256]{1,0:T(8,128)S(1)} %broadcast_multiply_fusion.2), kind=kOutput, calls=%fused_computation.34 | convolution fusion | flops 387317760 | bytes 4129792 | tf_op jit(solution)/shard_map/bmd,bmn->dn/dot_general | solution.py:45
  174.0 10.6 %fusion.14 = (f32[1280]{0:T(1024)S(1)}, f32[6,256]{1,0:T(8,128)S(1)}, f32[6,256]{1,0:T(8,128)S(1)}, f32[6,256,1280]{2,1,0:T(8,128)}) fusion(bf16[6,256,1280]{2,1,0:T(8,128)(2,1)} %param.6, f32[6,256]{1,0:T(8,128)S(1)} %add_rsqrt_fusion, f32[6,256]{1,0:T(8,128)S(1)} %broadcast_multiply_fusion.2, f32[1280]{0:T(1024)S(1)} %copy-done.7, ...), kind=kOutput, calls=%fused_computation.16 | convolution fusion | flops 397143808 | bytes 19834880 | tf_op jit(solution)/shard_map/bmn,dn->bmd/dot_general | solution.py:42
  184.7 86.7 %all-reduce.3.cloned.1.call-done = f32[1280,16]{0,1:T(8,128)} async-done(((f32[1280,16]{0,1:T(8,128)}), f32[1280,16]{0,1:T(8,128)}) %all-reduce.3.cloned.1.call-update) | async-done | bytes 81936 | tf_op jit(solution)/shard_map/psum | solution.py:115
  271.3 8.4 %fusion.13 = bf16[6,256,1280]{2,1,0:T(8,128)(2,1)} fusion(bf16[6,256,1280]{2,1,0:T(8,128)(2,1)} %param.6, bf16[6,256,1280]{2,1,0:T(8,128)(2,1)} %param.7, f32[6,256,1280]{2,1,0:T(8,128)} %get-tuple-element.18, f32[6,256]{1,0:T(8,128)S(1)} %get-tuple-element.19, f32[6,256]{1,0:T(8,128)S(1)} %get-tuple-element.20, f32[1280]{0:T(1024)S(1)} %copy-done.7, ...), kind=kLoop, calls=%fused_computation.15 | loop fusion | flops 21626880 | bytes 19690496 | tf_op jit(solution)/shard_map/convert_element_type | solution.py:114
  279.7 32.9 %psum.28 = f32[1280]{0:T(1024)S(1)} all-reduce(f32[1280]{0:T(1024)S(1)} %get-tuple-element.5), channel_id=1, replica_groups=mesh['dp'=2,'expert'=8,'tensor'=2] {'expert','tensor'}, use_global_device_ids=true, to_apply=%region_13.0 | all-reduce | flops 1280 | bytes 10240 | tf_op jit(solution)/shard_map/psum | solution.py:115
  312.6 5.6 %psum.29 = f32[1280]{0:T(1024)} all-reduce(f32[1280]{0:T(1024)S(1)} %psum.28), channel_id=1, replica_groups=mesh['dp'=2,'expert'=8,'tensor'=2] {'dp'}, use_global_device_ids=true, to_apply=%region_14.0 | all-reduce | flops 1280 | bytes 10240 | tf_op jit(solution)/shard_map/psum | solution.py:115
  (56 shorter events, 29.6 us)
Async XLA Ops:
  7.2 59.2 %copy-start = (bf16[1,1280,1280]{2,1,0:T(8,128)(2,1)S(1)}, bf16[1,1280,1280]{2,1,0:T(8,128)(2,1)}, u32[]{:S(2)}) copy-start(bf16[1,1280,1280]{2,1,0:T(8,128)(2,1)} %param.10) | copy-start | bytes 9830404
  7.2 6.3 %copy-start.1 = (bf16[6,256,1280]{2,1,0:T(8,128)(2,1)S(1)}, bf16[6,256,1280]{2,1,0:T(8,128)(2,1)}, u32[]{:S(2)}) copy-start(bf16[6,256,1280]{2,1,0:T(8,128)(2,1)} %param.6) | copy-start | bytes 11796484
  7.2 6.3 %copy-start.6 = (f32[1280]{0:T(1024)S(1)}, f32[1280]{0:T(1024)}, u32[]{:S(2)}) copy-start(f32[1280]{0:T(1024)} %param.8) | copy-start | bytes 15364
  7.2 6.3 %copy-start.4 = (bf16[1280,16]{0,1:T(8,128)(2,1)S(1)}, bf16[1280,16]{0,1:T(8,128)(2,1)}, u32[]{:S(2)}) copy-start(bf16[1280,16]{0,1:T(8,128)(2,1)} %param.9) | copy-start | bytes 122884
  15.1 0.8 copy-start.3
  22.0 15.7 %all-to-all-start.1 = ((bf16[6,8,2,1280]{3,2,0,1:T(2,128)(2,1)}), bf16[6,8,2,1280]{3,2,0,1:T(2,128)(2,1)S(1)}, u32[]{:S(2)}, u32[]{:S(2)}) async-start(bf16[6,8,2,1280]{3,2,0,1:T(2,128)(2,1)} %copy.39), calls=%async_computation.1 | async-start | bytes 491520 | tf_op jit(solution)/shard_map/all_to_all | solution.py:74
  37.7 15.6 %all-to-all-start = ((bf16[6,8,2,1280]{3,2,0,1:T(2,128)(2,1)}), bf16[6,8,2,1280]{3,2,0,1:T(2,128)(2,1)}, u32[]{:S(2)}, u32[]{:S(2)}) async-start(bf16[6,8,2,1280]{3,2,0,1:T(2,128)(2,1)} %copy.37), calls=%async_computation | async-start | bytes 491520 | tf_op jit(solution)/shard_map/all_to_all | solution.py:99
  42.2 87.4 %reduce-scatter.3.cloned.1.call-start = ((), (), s32[]{:S(2)}) async-start(), calls=%async_computation.8 | async-start | bytes 1474560 | tf_op jit(solution)/shard_map/reduce_scatter | solution.py:104
  72.5 0.8 copy-start.2
  75.5 66.7 %reduce-scatter.5.cloned.1.call-start = ((), (), s32[]{:S(2)}) async-start(), calls=%async_computation.9 | async-start | bytes 1474560 | tf_op jit(solution)/shard_map/reduce_scatter | solution.py:81
  85.6 22.0 %all-to-all-start.4 = ((bf16[192,2,640]{2,0,1:T(8,128)(2,1)}), bf16[192,2,640]{2,0,1:T(8,128)(2,1)}, u32[]{:S(2)}, u32[]{:S(2)}) async-start(bf16[192,2,640]{2,0,1:T(8,128)(2,1)} %copy.45), calls=%async_computation.6 | async-start | bytes 983040 | tf_op jit(solution)/shard_map/all_to_all | solution.py:117
  107.5 23.9 %all-to-all-start.5 = ((bf16[192,2,640]{2,0,1:T(8,128)(2,1)}), bf16[192,2,640]{2,0,1:T(8,128)(2,1)}, u32[]{:S(2)}, u32[]{:S(2)}) async-start(bf16[192,2,640]{2,0,1:T(8,128)(2,1)} %copy.46), calls=%async_computation.7 | async-start | bytes 983040 | tf_op jit(solution)/shard_map/all_to_all | solution.py:118
  131.4 14.3 %all-to-all-start.2 = ((bf16[48,1,2,1280]{3,2,1,0:T(2,128)(2,1)}), bf16[48,1,2,1280]{3,2,1,0:T(2,128)(2,1)S(1)}, u32[]{:S(2)}, u32[]{:S(2)}) async-start(bf16[48,1,2,1280]{3,2,1,0:T(2,128)(2,1)} %bitcast.85), calls=%async_computation.3 | async-start | bytes 491520 | tf_op jit(solution)/shard_map/all_to_all | solution.py:108
  145.7 16.5 %all-to-all-start.3 = ((bf16[48,1,2,1280]{3,2,1,0:T(2,128)(2,1)}), bf16[48,1,2,1280]{3,2,1,0:T(2,128)(2,1)}, u32[]{:S(2)}, u32[]{:S(2)}) async-start(bf16[48,1,2,1280]{3,2,1,0:T(2,128)(2,1)} %bitcast.86), calls=%async_computation.5 | async-start | bytes 491520 | tf_op jit(solution)/shard_map/all_to_all | solution.py:88
  150.8 120.5 %all-reduce.3.cloned.1.call-start = ((), (), s32[]{:S(2)}) async-start(), calls=%async_computation.10 | async-start | bytes 163840 | tf_op jit(solution)/shard_map/psum | solution.py:115
  168.3 5.6 %copy-start.5 = (bf16[1280,16]{0,1:T(8,128)(2,1)S(1)}, bf16[1280,16]{0,1:T(8,128)(2,1)}, u32[]{:S(2)}) copy-start(bf16[1280,16]{0,1:T(8,128)(2,1)} %param.9) | copy-start | bytes 122884
  168.3 5.6 %copy-start.7 = (f32[1280]{0:T(1024)S(1)}, f32[1280]{0:T(1024)}, u32[]{:S(2)}) copy-start(f32[1280]{0:T(1024)} %param.8) | copy-start | bytes 15364
  184.6 133.6 %all-reduce.5.cloned.1.call-start = ((), (), s32[]{:S(2)}) async-start(), calls=%async_computation.11 | async-start | bytes 163840 | tf_op jit(solution)/shard_map/psum | solution.py:115
Sparse Core Ops, SparseCore 0:
  75.6 19.4 reduce-scatter.2
  98.0 19.6 reduce-scatter.4
  184.7 86.5 all-reduce.2
  273.4 21.9 all-reduce.4
